TPU v7x, 32 devices: a whole 2x2x4 slice. The times are simulated.
32 devices in a mesh: dp: 16 (over z, y, x), mp: 2 (over core).
Axes of the slice: x: 2, y: 2, z: 4, core: 2. Of those that a mesh axis runs over, the one named last changes fastest.
Arguments:
- hidden_state: bfloat16 [32, 19, 19, 256], P('dp'), may hold values from -6 to 6
- actions: int32 [32, 2], P('dp'), may hold values from 0 to 361
- value_target: int32 [32, 2], P('dp'), may hold values from 0 to 600
- reward_target: int32 [32, 2], P('dp'), may hold values from 0 to 600
- kernel_first: float32 [3, 3, 256, 256], P(None, None, 'dp', 'mp'), may hold values from -6 to 6
- kernel_second: float32 [3, 3, 256, 256], P(None, None, 'dp', 'mp'), may hold values from -6 to 6
- head_weight: float32 [2, 256, 601], P('mp', 'dp'), may hold values from -6 to 6
- action_embed: float32 [2, 256], P('mp', 'dp'), may hold values from -6 to 6
- first_mean: float32 [3, 3, 256, 256], P(None, None, 'dp', 'mp'), may hold values from -0.00061035156 to 0.00061035156
- first_square: float32 [3, 3, 256, 256], P(None, None, 'dp', 'mp'), may hold values from 1e-09 to 1e-06
- second_mean: float32 [3, 3, 256, 256], P(None, None, 'dp', 'mp'), may hold values from -0.00061035156 to 0.00061035156
- second_square: float32 [3, 3, 256, 256], P(None, None, 'dp', 'mp'), may hold values from 1e-09 to 1e-06
- head_mean: float32 [2, 256, 601], P('mp', 'dp'), may hold values from -0.0029296875 to 0.0029296875
- head_square: float32 [2, 256, 601], P('mp', 'dp'), may hold values from 1e-08 to 1e-06
- embed_mean: float32 [2, 256], P('mp', 'dp'), may hold values from -0.0017089844 to 0.0017089844
- embed_square: float32 [2, 256], P('mp', 'dp'), may hold values from 1e-09 to 1e-06
Outputs:
- kernel_first_new: float32 [3, 3, 256, 256], P(None, None, 'dp', 'mp')
- kernel_second_new: float32 [3, 3, 256, 256], P(None, None, 'dp', 'mp')
- head_weight_new: float32 [2, 256, 601], P('mp', 'dp')
- action_embed_new: float32 [2, 256], P('mp', 'dp')
- first_mean_new: float32 [3, 3, 256, 256], P(None, None, 'dp', 'mp')
- first_square_new: float32 [3, 3, 256, 256], P(None, None, 'dp', 'mp')
- second_mean_new: float32 [3, 3, 256, 256], P(None, None, 'dp', 'mp')
- second_square_new: float32 [3, 3, 256, 256], P(None, None, 'dp', 'mp')
- head_mean_new: float32 [2, 256, 601], P('mp', 'dp')
- head_square_new: float32 [2, 256, 601], P('mp', 'dp')
- embed_mean_new: float32 [2, 256], P('mp', 'dp')
- embed_square_new: float32 [2, 256], P('mp', 'dp')
- first_grad: float32 [3, 3, 256, 256], P(None, None, 'dp', 'mp')
- second_grad: float32 [3, 3, 256, 256], P(None, None, 'dp', 'mp')
- head_grad: float32 [2, 256, 601], P('mp', 'dp')
- embed_grad: float32 [2, 256], P('mp', 'dp')
Inputs may be any that keep to these rules, and one draw needn't show every extreme that they name: `actions`: the value 361 stands for a pass.
All inputs are finite; a program needn't handle non-finite values.
Results may differ from a plain program's by a relative error of at most 0.02.
Values may be sent and summed in bfloat16 or wider, within the bound.
No kernel may reach another device: no remote copies, remote signals or barrier semaphores. Data moves between devices by JAX's collectives and lax.ppermute only.
A program may use at most 64 MiB of HBM per device.

v0:
```python
import jax
import jax.numpy as jnp
from jax import lax
from jax.sharding import PartitionSpec as P

CHANNELS = 256
head_scale = 4.0
soft_cap = 15.0
eps_norm = 1e-05
beta_one = 0.9
beta_two = 0.999
step_size = 0.1
eps_adam = 1e-08


def conv_apply(field, kernel, layout):
    return lax.conv_general_dilated(
        field,
        kernel,
        (1, 1),
        "SAME",
        dimension_numbers=("NHWC", layout, "NHWC"),
        preferred_element_type=jnp.float32,
    )


def gate_slope(pre):
    sig = jax.nn.sigmoid(pre)
    return sig * (1.0 + pre * (1.0 - sig))


def tap_products(field, grad, field_rows):
    side = field.shape[1]
    padded = jnp.pad(field, ((0, 0), (1, 1), (1, 1), (0, 0)))
    flat_grad = grad.reshape(-1, grad.shape[3])
    blocks = []
    for offset in range(9):
        row_start = offset // 3
        col_start = offset % 3
        window = padded[:, row_start : row_start + side, col_start : col_start + side, :].reshape(
            -1, field.shape[3]
        )
        if field_rows:
            blocks.append(
                lax.dot_general(
                    window, flat_grad, (((0,), (0,)), ((), ())), preferred_element_type=jnp.float32
                )
            )
        else:
            blocks.append(
                lax.dot_general(
                    flat_grad, window, (((0,), (0,)), ((), ())), preferred_element_type=jnp.float32
                )
            )
    stacked = jnp.stack(blocks)
    return stacked.reshape(3, 3, stacked.shape[1], stacked.shape[2])


def action_planes(move, board):
    cells = board * board
    plane = (lax.broadcasted_iota(jnp.int32, (move.shape[0], cells), 1) == move[:, None]).astype(
        jnp.float32
    )
    passed = (move == cells).astype(jnp.float32)
    return (plane.reshape(move.shape[0], board, board, 1), passed[:, None, None, None])


def head_backward(state, head_used, value_now, reward_now, total):
    pooled = jnp.mean(state, axis=(1, 2)).astype(jnp.bfloat16)
    raw = head_scale * jnp.stack(
        [
            jnp.dot(pooled, head_used[0], preferred_element_type=jnp.float32),
            jnp.dot(pooled, head_used[1], preferred_element_type=jnp.float32),
        ]
    )
    squashed = jnp.tanh(raw / soft_cap)
    raised = jnp.exp(soft_cap * squashed)
    chances = raised / jnp.sum(raised, axis=2, keepdims=True)
    targets = jnp.stack([value_now, reward_now])
    picked = (lax.broadcasted_iota(jnp.int32, raw.shape, 2) == targets[:, :, None]).astype(
        jnp.float32
    )
    logit_grad = ((chances - picked) * (1.0 - squashed * squashed) / total).astype(jnp.bfloat16)
    pooled_grad = head_scale * (
        jnp.dot(logit_grad[0], head_used[0].T, preferred_element_type=jnp.float32)
        + jnp.dot(logit_grad[1], head_used[1].T, preferred_element_type=jnp.float32)
    )
    return (pooled, logit_grad, pooled_grad)


def adam_update(param, grad, mean, square):
    mean_new = beta_one * mean + (1.0 - beta_one) * grad
    square_new = beta_two * square + (1.0 - beta_two) * grad * grad
    param_new = param - step_size * mean_new / (jnp.sqrt(square_new) + eps_adam)
    return (param_new, mean_new, square_new)


def local(
    hidden_state,
    actions,
    value_target,
    reward_target,
    kernel_first,
    kernel_second,
    head_weight,
    action_embed,
    first_mean,
    first_square,
    second_mean,
    second_square,
    head_mean,
    head_square,
    embed_mean,
    embed_square,
):
    total = hidden_state.shape[0] * lax.axis_size("dp")
    board = hidden_state.shape[1]
    cells = board * board
    scale = (9.0 * CHANNELS) ** (-0.5)
    first_used, second_used, head_used, embed_used = (
        lax.all_gather(kernel_first.astype(jnp.bfloat16), "dp", axis=2, tiled=True),
        lax.all_gather(kernel_second.astype(jnp.bfloat16), "dp", axis=2, tiled=True),
        lax.all_gather(head_weight.astype(jnp.bfloat16), "dp", axis=1, tiled=True),
        lax.all_gather(action_embed.astype(jnp.bfloat16), "dp", axis=1, tiled=True),
    )
    first_used, second_used, head_used, embed_used = (
        lax.all_gather(first_used, "mp", axis=3, tiled=True),
        lax.all_gather(second_used, "mp", axis=3, tiled=True),
        lax.all_gather(head_used, "mp", axis=0, tiled=True),
        lax.all_gather(embed_used, "mp", axis=0, tiled=True),
    )
    count = hidden_state.shape[0] // lax.axis_size("mp")
    begin = lax.axis_index("mp") * count
    states = lax.dynamic_slice_in_dim(hidden_state, begin, count, 0)
    moves = lax.dynamic_slice_in_dim(actions, begin, count, 0)
    values = lax.dynamic_slice_in_dim(value_target, begin, count, 0)
    rewards = lax.dynamic_slice_in_dim(reward_target, begin, count, 0)
    unroll = moves.shape[1]
    embed = embed_used.astype(jnp.float32)
    state = states.astype(jnp.float32)
    saved = []
    for position in range(unroll):
        plane, passed = action_planes(moves[:, position], board)
        mixed = state + plane * embed[0] + passed * embed[1]
        conv_input = mixed.astype(jnp.bfloat16)
        pre = scale * conv_apply(conv_input, first_used, "HWIO")
        hidden = jax.nn.silu(pre).astype(jnp.bfloat16)
        branch = conv_apply(hidden, second_used, "HWOI")
        summed = mixed + scale * branch
        factor = lax.rsqrt(jnp.mean(summed * summed, axis=(1, 2, 3), keepdims=True) + eps_norm)
        state = summed * factor
        pooled, logit_grad, pooled_grad = head_backward(
            state, head_used, values[:, position], rewards[:, position], total
        )
        saved.append(
            (
                plane,
                passed,
                conv_input,
                pre,
                hidden,
                summed,
                factor,
                pooled,
                logit_grad,
                pooled_grad,
            )
        )
    first_grad = jnp.zeros(first_used.shape, jnp.float32)
    second_grad = jnp.zeros(second_used.shape, jnp.float32)
    head_grad = jnp.zeros(head_used.shape, jnp.float32)
    embed_grad = jnp.zeros(embed_used.shape, jnp.float32)
    carry = jnp.zeros(states.shape, jnp.float32)
    for position in range(unroll - 1, -1, -1):
        plane, passed, conv_input, pre, hidden, summed, factor, pooled, logit_grad, pooled_grad = (
            saved[position]
        )
        state_grad = carry + pooled_grad[:, None, None, :] / cells
        summed_grad = factor * state_grad - factor * factor * factor * summed * jnp.mean(
            state_grad * summed, axis=(1, 2, 3), keepdims=True
        )
        branch_grad = summed_grad.astype(jnp.bfloat16)
        hidden_grad = scale * conv_apply(branch_grad, second_used[::-1, ::-1], "HWIO")
        inner_grad = (hidden_grad * gate_slope(pre)).astype(jnp.bfloat16)
        input_grad = conv_apply(inner_grad, first_used[::-1, ::-1], "HWOI")
        carry = summed_grad + scale * input_grad
        first_grad = first_grad + scale * tap_products(conv_input, inner_grad, True)
        second_grad = second_grad + scale * tap_products(hidden, branch_grad, False)
        head_grad = head_grad + head_scale * jnp.stack(
            [
                lax.dot_general(
                    pooled,
                    logit_grad[0],
                    (((0,), (0,)), ((), ())),
                    preferred_element_type=jnp.float32,
                ),
                lax.dot_general(
                    pooled,
                    logit_grad[1],
                    (((0,), (0,)), ((), ())),
                    preferred_element_type=jnp.float32,
                ),
            ]
        )
        embed_grad = embed_grad + jnp.stack(
            [jnp.sum(plane * carry, axis=(0, 1, 2)), jnp.sum(passed * carry, axis=(0, 1, 2))]
        )
    first_grad, second_grad, head_grad, embed_grad = (
        lax.psum_scatter(first_grad, "mp", scatter_dimension=3, tiled=True),
        lax.psum_scatter(second_grad, "mp", scatter_dimension=3, tiled=True),
        lax.psum_scatter(head_grad, "mp", scatter_dimension=0, tiled=True),
        lax.psum_scatter(embed_grad, "mp", scatter_dimension=0, tiled=True),
    )
    first_grad, second_grad, head_grad, embed_grad = (
        lax.psum_scatter(first_grad, "dp", scatter_dimension=2, tiled=True),
        lax.psum_scatter(second_grad, "dp", scatter_dimension=2, tiled=True),
        lax.psum_scatter(head_grad, "dp", scatter_dimension=1, tiled=True),
        lax.psum_scatter(embed_grad, "dp", scatter_dimension=1, tiled=True),
    )
    first_new, first_mean_new, first_square_new = adam_update(
        kernel_first, first_grad, first_mean, first_square
    )
    second_new, second_mean_new, second_square_new = adam_update(
        kernel_second, second_grad, second_mean, second_square
    )
    head_new, head_mean_new, head_square_new = adam_update(
        head_weight, head_grad, head_mean, head_square
    )
    embed_new, embed_mean_new, embed_square_new = adam_update(
        action_embed, embed_grad, embed_mean, embed_square
    )
    return (
        first_new,
        second_new,
        head_new,
        embed_new,
        first_mean_new,
        first_square_new,
        second_mean_new,
        second_square_new,
        head_mean_new,
        head_square_new,
        embed_mean_new,
        embed_square_new,
        first_grad,
        second_grad,
        head_grad,
        embed_grad,
    )


def solution(mesh):
    placed = (
        P("dp", None, None, None),
        P("dp", None),
        P("dp", None),
        P("dp", None),
        P(None, None, "dp", "mp"),
        P(None, None, "dp", "mp"),
        P("mp", "dp", None),
        P("mp", "dp"),
        P(None, None, "dp", "mp"),
        P(None, None, "dp", "mp"),
        P(None, None, "dp", "mp"),
        P(None, None, "dp", "mp"),
        P("mp", "dp", None),
        P("mp", "dp", None),
        P("mp", "dp"),
        P("mp", "dp"),
    )
    return jax.shard_map(
        local,
        mesh=mesh,
        in_specs=placed,
        out_specs=(
            P(None, None, "dp", "mp"),
            P(None, None, "dp", "mp"),
            P("mp", "dp", None),
            P("mp", "dp"),
            P(None, None, "dp", "mp"),
            P(None, None, "dp", "mp"),
            P(None, None, "dp", "mp"),
            P(None, None, "dp", "mp"),
            P("mp", "dp", None),
            P("mp", "dp", None),
            P("mp", "dp"),
            P("mp", "dp"),
            P(None, None, "dp", "mp"),
            P(None, None, "dp", "mp"),
            P("mp", "dp", None),
            P("mp", "dp"),
        ),
        check_vma=False,
    )
```

profile of v0, /device:TPU:0, one launch (start us, length us, event | category | flops | bytes accessed | tf_op | source)
XLA Modules:
  0.0 581.1 jit_solution(16968905555778703401)
XLA Ops:
  7.3 1.0 convert_element_type.150
  8.3 48.3 %all_gather.26 = bf16[3,3,256,128]{3,2,1,0:T(8,128)(2,1)} all-gather(bf16[3,3,16,128]{3,2,1,0:T(8,128)(2,1)S(1)} %convert_element_type.150), channel_id=1, replica_groups=mesh['dp'=16,'mp'=2] {'dp'}, dimensions={2}, use_global_device_ids=true | all-gather | bytes 626688 | tf_op jit(solution)/shard_map/all_gather | solution.py:121
  56.6 0.9 convert_element_type.152
  57.5 41.0 %all_gather.28 = bf16[3,3,256,128]{3,2,1,0:T(8,128)(2,1)} all-gather(bf16[3,3,16,128]{3,2,1,0:T(8,128)(2,1)S(1)} %convert_element_type.152), channel_id=1, replica_groups=mesh['dp'=16,'mp'=2] {'dp'}, dimensions={2}, use_global_device_ids=true | all-gather | bytes 626688 | tf_op jit(solution)/shard_map/all_gather | solution.py:122
  100.1 38.8 %all-reduce.4 = bf16[256]{0:T(256)(128)(2,1)S(1)} all-reduce(bf16[256]{0:T(256)(128)(2,1)S(1)} %dynamic-update-slice), channel_id=1, replica_groups=mesh['dp'=16,'mp'=2] {'dp'}, use_global_device_ids=true, to_apply=%add.4 | all-reduce | flops 256 | bytes 1024
  138.9 1.8 all-gather
  144.4 37.2 %all_gather.30 = bf16[1,256,601]{2,1,0:T(8,128)(2,1)S(1)} all-gather(bf16[1,16,601]{2,1,0:T(8,128)(2,1)S(1)} %convert_element_type.157), channel_id=1, replica_groups=mesh['dp'=16,'mp'=2] {'dp'}, dimensions={1}, use_global_device_ids=true | all-gather | bytes 326944 | tf_op jit(solution)/shard_map/all_gather | solution.py:123
  183.4 1.4 add_reduce_fusion
  184.8 1.4 add_reduce_fusion.1
  186.2 2.4 all_gather.31
  188.6 0.8 fusion.61
  189.5 2.0 fusion.6
  192.3 2.0 convolution_multiply_fusion.3
  194.8 0.8 multiply_reduce_fusion.8
  197.4 2.1 fusion.5
  199.5 0.8 select_bitcast_fusion.2
  201.7 0.8 multiply_reduce_fusion.7
  207.8 2.1 fusion.7
  211.9 0.8 multiply_reduce_fusion.3
  213.3 0.8 fusion.348
  214.2 1.0 pad.29
  216.4 1.2 fusion
  218.3 1.2 fusion.17
  219.6 1.2 fusion.16
  220.8 1.3 fusion.15
  222.1 1.2 fusion.14
  223.4 1.2 fusion.13
  224.6 1.2 fusion.12
  225.9 1.2 fusion.11
  227.1 1.3 fusion.10
  228.4 1.2 fusion.9
  229.8 0.9 reshape.830
  230.6 1.0 slice_bitcast_fusion.9
  231.6 1.2 fusion.26
  235.6 2.0 add_multiply_fusion
  237.7 0.8 copy-done.8
  238.7 2.0 fusion.8
  247.1 1.7 add_multiply_fusion.1
  251.8 2.5 all-reduce.5
  254.9 0.8 copy.106
  257.3 1.5 reduce-scatter.10.cloned.1.call-done
  258.8 80.4 %reduce-scatter.22.cloned.1.call-done = f32[16,1]{1,0:T(8,128)} async-done(((f32[256,1]{1,0:T(8,128)}), f32[16,1]{1,0:T(8,128)}) %reduce-scatter.22.cloned.1.call-update) | async-done | bytes 80
  340.5 75.6 %reduce-scatter.20.cloned.1.call-done = f32[1,16,601]{2,1,0:T(8,128)} async-done(((f32[1,256,601]{2,1,0:T(8,128)}), f32[1,16,601]{2,1,0:T(8,128)}) %reduce-scatter.20.cloned.1.call-update) | async-done | bytes 38480 | tf_op jit(solution)/shard_map/reduce_scatter | solution.py:217
  416.1 1.4 divide_subtract_fusion.2
  417.6 77.1 %reduce-scatter.16.cloned.1.call-done = f32[3,3,16,128]{3,2,1,0:T(8,128)} async-done(((f32[3,3,256,128]{3,2,1,0:T(8,128)}), f32[3,3,16,128]{3,2,1,0:T(8,128)}) %reduce-scatter.16.cloned.1.call-update) | async-done | bytes 73744 | tf_op jit(solution)/shard_map/reduce_scatter | solution.py:216
  494.6 1.6 divide_subtract_fusion
  496.2 76.8 %reduce-scatter.12.cloned.1.call-done = f32[3,3,16,128]{3,2,1,0:T(8,128)} async-done(((f32[3,3,256,128]{3,2,1,0:T(8,128)}), f32[3,3,16,128]{3,2,1,0:T(8,128)}) %reduce-scatter.12.cloned.1.call-update) | async-done | bytes 73744 | tf_op jit(solution)/shard_map/reduce_scatter | solution.py:215
  573.0 1.6 divide_subtract_fusion.1
  (222 shorter events, 31.9 us)
Async XLA Ops:
  7.2 136.1 %copy-start = (bf16[2,19,19,256]{3,0,2,1:T(2,128)(2,1)S(1)}, bf16[2,19,19,256]{3,0,2,1:T(2,128)(2,1)}, u32[]{:S(2)}) copy-start(bf16[2,19,19,256]{3,0,2,1:T(2,128)(2,1)} %param.16) | copy-start | bytes 1108996
  7.2 91.4 %copy-start.38 = (u32[32]{0:T(128)S(1)}, u32[32]{0:T(128)}, u32[]{:S(2)}) copy-start(u32[32]{0:T(128)} %constant.145) | copy-start | bytes 388
  7.2 91.4 %copy-start.28 = (f32[1,16]{1,0:T(1,128)S(1)}, f32[1,16]{1,0:T(1,128)}, u32[]{:S(2)}) copy-start(f32[1,16]{1,0:T(1,128)} %param.23) | copy-start | bytes 196
  7.2 133.5 %copy-start.36 = (s32[2,2]{1,0:T(2,128)S(1)}, s32[2,2]{1,0:T(2,128)}, u32[]{:S(2)}) copy-start(s32[2,2]{1,0:T(2,128)} %param.17) | copy-start | bytes 52
  7.2 137.1 %copy-start.17 = (f32[1,16,601]{2,1,0:T(8,128)S(1)}, f32[1,16,601]{2,1,0:T(8,128)}, u32[]{:S(2)}) copy-start(f32[1,16,601]{2,1,0:T(8,128)} %param.22) | copy-start | bytes 115396
  7.2 174.4 %copy-start.32 = (s32[2,2]{1,0:T(2,128)S(1)}, s32[2,2]{1,0:T(2,128)}, u32[]{:S(2)}) copy-start(s32[2,2]{1,0:T(2,128)} %param.18) | copy-start | bytes 52
  7.3 174.4 %copy-start.31 = (s32[2,2]{1,0:T(2,128)S(1)}, s32[2,2]{1,0:T(2,128)}, u32[]{:S(2)}) copy-start(s32[2,2]{1,0:T(2,128)} %param.19) | copy-start | bytes 52
  7.3 182.2 %all-gather.4.cloned.1.call-start = ((), (), s32[]{:S(2)}) async-start(), calls=%async_computation.7 | async-start | bytes 1769472 | tf_op jit(solution)/shard_map/all_gather | solution.py:127
  56.6 135.1 %all-gather.6.cloned.1.call-start = ((), (), s32[]{:S(2)}) async-start(), calls=%async_computation.8 | async-start | bytes 1769472 | tf_op jit(solution)/shard_map/all_gather | solution.py:128
  98.5 157.2 %reduce-scatter.18.cloned.1.call-start = ((), (), s32[]{:S(2)}) async-start(), calls=%async_computation.13 | async-start | bytes 1966080 | tf_op jit(solution)/shard_map/reduce_scatter | solution.py:211
  181.6 7.9 %copy-start.26 = (pred[8,3]{0,1:T(4,128)(4,1)S(1)}, pred[8,3]{0,1:T(4,128)(4,1)}, u32[]{:S(2)}) copy-start(pred[8,3]{0,1:T(4,128)(4,1)} %constant.135) | copy-start | bytes 76
  191.5 0.8 copy-start.9
  196.4 0.7 copy-start.1
  197.4 3.0 copy-start.35
  199.5 0.9 copy-start.11
  204.5 3.3 copy-start.12
  207.8 2.8 copy-start.33
  209.9 0.7 copy-start.5
  215.3 2.3 copy-start.7
  217.7 38.8 %reduce-scatter.14.cloned.1.call-start = ((), (), s32[]{:S(2)}) async-start(), calls=%async_computation.11 | async-start | bytes 3538944 | tf_op jit(solution)/shard_map/reduce_scatter | solution.py:210
  227.1 2.5 copy-start.3
  230.6 2.2 copy-start.16
  233.2 0.9 copy-start.4
  237.6 0.9 copy-start.8
  237.6 1.1 copy-start.10
  237.6 1.2 copy-start.19
  237.6 3.1 copy-start.6
  237.6 3.8 copy-start.15
  237.6 21.2 %reduce-scatter.10.cloned.1.call-start = ((), (), s32[]{:S(2)}) async-start(), calls=%async_computation.9 | async-start | bytes 3538944 | tf_op jit(solution)/shard_map/reduce_scatter | solution.py:209
  243.5 1.0 copy-start.2
  248.8 0.7 copy-start.37
  248.8 1.4 copy-start.34
  248.9 90.3 %reduce-scatter.22.cloned.1.call-start = ((), (), s32[]{:S(2)}) async-start(), calls=%async_computation.15 | async-start | bytes 139264
  251.5 88.5 %copy-start.29 = (f32[1,16]{1,0:T(1,128)S(1)}, f32[1,16]{1,0:T(1,128)}, u32[]{:S(2)}) copy-start(f32[1,16]{1,0:T(1,128)} %param.30) | copy-start | bytes 196
  251.5 88.5 %copy-start.30 = (f32[1,16]{1,0:T(1,128)S(1)}, f32[1,16]{1,0:T(1,128)}, u32[]{:S(2)}) copy-start(f32[1,16]{1,0:T(1,128)} %param.31) | copy-start | bytes 196
  251.5 164.7 %copy-start.18 = (f32[1,16,601]{2,1,0:T(8,128)S(1)}, f32[1,16,601]{2,1,0:T(8,128)}, u32[]{:S(2)}) copy-start(f32[1,16,601]{2,1,0:T(8,128)} %param.22) | copy-start | bytes 115396
  251.5 164.6 %copy-start.24 = (f32[1,16,601]{2,1,0:T(8,128)S(1)}, f32[1,16,601]{2,1,0:T(8,128)}, u32[]{:S(2)}) copy-start(f32[1,16,601]{2,1,0:T(8,128)} %param.28) | copy-start | bytes 115396
  251.5 164.6 %copy-start.25 = (f32[1,16,601]{2,1,0:T(8,128)S(1)}, f32[1,16,601]{2,1,0:T(8,128)}, u32[]{:S(2)}) copy-start(f32[1,16,601]{2,1,0:T(8,128)} %param.29) | copy-start | bytes 115396
  251.5 243.1 %copy-start.13 = (f32[3,3,16,128]{3,2,1,0:T(8,128)S(1)}, f32[3,3,16,128]{3,2,1,0:T(8,128)}, u32[]{:S(2)}) copy-start(f32[3,3,16,128]{3,2,1,0:T(8,128)} %param.21) | copy-start | bytes 221188
  251.5 243.1 %copy-start.20 = (f32[3,3,16,128]{3,2,1,0:T(8,128)S(1)}, f32[3,3,16,128]{3,2,1,0:T(8,128)}, u32[]{:S(2)}) copy-start(f32[3,3,16,128]{3,2,1,0:T(8,128)} %param.26) | copy-start | bytes 221188
  251.5 243.1 %copy-start.21 = (f32[3,3,16,128]{3,2,1,0:T(8,128)S(1)}, f32[3,3,16,128]{3,2,1,0:T(8,128)}, u32[]{:S(2)}) copy-start(f32[3,3,16,128]{3,2,1,0:T(8,128)} %param.27) | copy-start | bytes 221188
  251.5 321.5 %copy-start.14 = (f32[3,3,16,128]{3,2,1,0:T(8,128)S(1)}, f32[3,3,16,128]{3,2,1,0:T(8,128)}, u32[]{:S(2)}) copy-start(f32[3,3,16,128]{3,2,1,0:T(8,128)} %param.20) | copy-start | bytes 221188
  251.6 321.5 %copy-start.22 = (f32[3,3,16,128]{3,2,1,0:T(8,128)S(1)}, f32[3,3,16,128]{3,2,1,0:T(8,128)}, u32[]{:S(2)}) copy-start(f32[3,3,16,128]{3,2,1,0:T(8,128)} %param.24) | copy-start | bytes 221188
  251.6 321.4 %copy-start.23 = (f32[3,3,16,128]{3,2,1,0:T(8,128)S(1)}, f32[3,3,16,128]{3,2,1,0:T(8,128)}, u32[]{:S(2)}) copy-start(f32[3,3,16,128]{3,2,1,0:T(8,128)} %param.25) | copy-start | bytes 221188
  255.7 160.4 %reduce-scatter.20.cloned.1.call-start = ((), (), s32[]{:S(2)}) async-start(), calls=%async_computation.14 | async-start | bytes 696320 | tf_op jit(solution)/shard_map/reduce_scatter | solution.py:217
  256.5 238.2 %reduce-scatter.16.cloned.1.call-start = ((), (), s32[]{:S(2)}) async-start(), calls=%async_computation.12 | async-start | bytes 1253376 | tf_op jit(solution)/shard_map/reduce_scatter | solution.py:216
  257.2 315.8 %reduce-scatter.12.cloned.1.call-start = ((), (), s32[]{:S(2)}) async-start(), calls=%async_computation.10 | async-start | bytes 1253376 | tf_op jit(solution)/shard_map/reduce_scatter | solution.py:215
  340.0 234.7 %copy-start.27 = (f32[1,16]{1,0:T(1,128)}, f32[1,16]{1,0:T(1,128)S(1)}, u32[]{:S(2)}) copy-start(f32[1,16]{1,0:T(1,128)S(1)} %copy.107) | copy-start | bytes 196
Sparse Core Ops, SparseCore 0:
  56.7 4.7 all-gather.3
  98.7 6.9 all-gather.5
  217.8 6.4 reduce-scatter.17
  237.7 7.6 reduce-scatter.13
  249.0 9.7 reduce-scatter.9
  260.9 78.2 reduce-scatter.21
  342.0 74.0 reduce-scatter.19
  419.0 75.6 reduce-scatter.15
  497.5 75.4 reduce-scatter.11
where the time goes:
time: 582 us; the launch traced here: 581 us
  waiting for transfers between devices  313 us (54%)
  blocking collectives  172 us (30%)
  matrix products  33.7 us (6%)
  other arithmetic  24.3 us (4%)
  between operations  19.6 us (3%)
  local copies, waits for them, and re-layouts  18.2 us (3%)
    unnamed x10, waiting for transfers between devices  81.8 us
    reduce_scatter x1, waiting for transfers between devices, local(): lax.psum_scatter(second_grad, 'dp', scatter_dimension=2, tiled=True)  77.1 us
    reduce_scatter x1, waiting for transfers between devices, local(): lax.psum_scatter(first_grad, 'dp', scatter_dimension=2, tiled=True)  76.8 us
    reduce_scatter x1, waiting for transfers between devices, local(): lax.psum_scatter(head_grad, 'dp', scatter_dimension=1, tiled=True)  75.6 us
    all_gather x1, blocking collectives, local(): lax.all_gather(kernel_first.astype(jnp.bfloat16), 'dp', axis=2, tiled=True)  48.3 us
    unnamed x2, blocking collectives  41.3 us
    all_gather x1, blocking collectives, local(): lax.all_gather(kernel_second.astype(jnp.bfloat16), 'dp', axis=2, tiled=True)  41 us
    all_gather x1, blocking collectives, local(): lax.all_gather(head_weight.astype(jnp.bfloat16), 'dp', axis=1, tiled=True)  37.2 us
  transfers between devices with their start and end apart: 9, of which 5 were waited for; matrix products, arithmetic and copies ran while one was open for 8% of the time, Pallas kernels for 0%

commit v1 on v0

--- a/solution.py
+++ b/solution.py
@@ -119,7 +119,12 @@
     scale = (9.0 * CHANNELS) ** (-0.5)
     first_used, second_used, head_used, embed_used = (
         lax.all_gather(kernel_first.astype(jnp.bfloat16), "dp", axis=2, tiled=True),
-        lax.all_gather(kernel_second.astype(jnp.bfloat16), "dp", axis=2, tiled=True),
+        jnp.concatenate(
+            lax.all_to_all(
+                jnp.stack([kernel_second.astype(jnp.bfloat16)] * lax.axis_size("dp")), "dp", 0, 0
+            ),
+            axis=2,
+        ),
         lax.all_gather(head_weight.astype(jnp.bfloat16), "dp", axis=1, tiled=True),
         lax.all_gather(action_embed.astype(jnp.bfloat16), "dp", axis=1, tiled=True),
     )

time: 582 us -> 556 us (0.955)
  blocking collectives: 172 us -> 134 us
    all_gather x1 -> x0, blocking collectives: 41 us -> none  [local(): lax.all_gather(kernel_second.astype(jnp.bfloat16), 'dp', axis=2, tiled=True)]
  transfers between devices with their start and end apart: 9 -> 10, of which waited for: 5 -> 6; matrix products, arithmetic and copies ran while one was open for 8% -> 9% of each run, Pallas kernels for 0% -> 0%
where the time goes in v1:
time: 556 us; the launch traced here: 555 us
  waiting for transfers between devices  318 us (57%)
  blocking collectives  134 us (24%)
  matrix products  33.9 us (6%)
  other arithmetic  24.2 us (4%)
  local copies, waits for them, and re-layouts  20.8 us (4%)
  between operations  19.7 us (4%)
    unnamed x10, waiting for transfers between devices  81.6 us
    reduce_scatter x1, waiting for transfers between devices, local(): lax.psum_scatter(second_grad, 'dp', scatter_dimension=2, tiled=True)  76.9 us
    reduce_scatter x1, waiting for transfers between devices, local(): lax.psum_scatter(first_grad, 'dp', scatter_dimension=2, tiled=True)  76.7 us
    reduce_scatter x1, waiting for transfers between devices, local(): lax.psum_scatter(head_grad, 'dp', scatter_dimension=1, tiled=True)  75.5 us
    all_gather x1, blocking collectives, local(): lax.all_gather(kernel_first.astype(jnp.bfloat16), 'dp', axis=2, tiled=True)  48.3 us
    unnamed x2, blocking collectives  44.5 us
    all_gather x1, blocking collectives, local(): lax.all_gather(head_weight.astype(jnp.bfloat16), 'dp', axis=1, tiled=True)  37.2 us
    dot_general x18, matrix products, tap_products(): lax.dot_general(flat_grad, window, (((0,), (0,)), ((), ())), preferred_el...  14.9 us
  transfers between devices with their start and end apart: 10, of which 6 were waited for; matrix products, arithmetic and copies ran while one was open for 9% of the time, Pallas kernels for 0%

profile of v1, /device:TPU:0, one launch (start us, length us, event | category | flops | bytes accessed | tf_op | source)
XLA Modules:
  0.0 555.1 jit_solution(12873333255535824534)
XLA Ops:
  7.3 0.9 convert_element_type.150
  8.2 48.3 %all_gather.23 = bf16[3,3,256,128]{3,2,1,0:T(8,128)(2,1)} all-gather(bf16[3,3,16,128]{3,2,1,0:T(8,128)(2,1)S(1)} %convert_element_type.150), channel_id=1, replica_groups=mesh['dp'=16,'mp'=2] {'dp'}, dimensions={2}, use_global_device_ids=true | all-gather | bytes 626688 | tf_op jit(solution)/shard_map/all_gather | solution.py:121
  56.5 0.9 convert_element_type.152
  57.4 0.9 stack.203
  58.3 3.7 all-to-all-start
  65.6 42.1 %all-reduce.4 = bf16[256]{0:T(256)(128)(2,1)S(1)} all-reduce(bf16[256]{0:T(256)(128)(2,1)S(1)} %dynamic-update-slice), channel_id=1, replica_groups=mesh['dp'=16,'mp'=2] {'dp'}, use_global_device_ids=true, to_apply=%add.4 | all-reduce | flops 256 | bytes 1024
  107.6 1.8 all-gather
  111.0 37.2 %all_gather.26 = bf16[1,256,601]{2,1,0:T(8,128)(2,1)S(1)} all-gather(bf16[1,16,601]{2,1,0:T(8,128)(2,1)S(1)} %convert_element_type.157), channel_id=1, replica_groups=mesh['dp'=16,'mp'=2] {'dp'}, dimensions={1}, use_global_device_ids=true | all-gather | bytes 326944 | tf_op jit(solution)/shard_map/all_gather | solution.py:128
  149.6 1.4 add_reduce_fusion
  151.0 1.4 add_reduce_fusion.1
  153.0 2.3 all_gather.27
  155.3 0.9 copy.93
  157.3 2.0 fusion.6
  161.2 2.0 all-gather.6.cloned.1.call-done
  163.3 2.0 convolution_multiply_fusion.3
  165.8 0.8 multiply_reduce_fusion.8
  168.4 2.1 fusion.5
  170.5 0.8 select_bitcast_fusion.2
  172.7 0.8 multiply_reduce_fusion.7
  178.8 2.1 fusion.7
  184.3 0.8 fusion.348
  185.2 1.0 pad.29
  187.4 1.2 fusion
  188.9 1.4 fusion.17
  190.3 1.3 fusion.16
  191.7 1.2 fusion.15
  192.9 1.2 fusion.14
  194.1 1.2 fusion.13
  195.4 1.3 fusion.12
  196.6 1.2 fusion.11
  197.9 1.3 fusion.10
  199.2 1.2 fusion.9
  200.6 0.9 reshape.840
  201.5 1.0 slice_bitcast_fusion.9
  202.5 1.2 fusion.26
  206.4 2.0 add_multiply_fusion
  208.6 0.8 copy-done.8
  209.6 2.0 fusion.8
  218.0 1.7 add_multiply_fusion.1
  222.6 2.5 all-reduce.5
  228.1 5.1 reduce-scatter.10.cloned.1.call-done
  233.2 80.2 %reduce-scatter.22.cloned.1.call-done = f32[16,1]{1,0:T(8,128)} async-done(((f32[256,1]{1,0:T(8,128)}), f32[16,1]{1,0:T(8,128)}) %reduce-scatter.22.cloned.1.call-update) | async-done | bytes 80
  314.7 75.5 %reduce-scatter.20.cloned.1.call-done = f32[1,16,601]{2,1,0:T(8,128)} async-done(((f32[1,256,601]{2,1,0:T(8,128)}), f32[1,16,601]{2,1,0:T(8,128)}) %reduce-scatter.20.cloned.1.call-update) | async-done | bytes 38480 | tf_op jit(solution)/shard_map/reduce_scatter | solution.py:222
  390.3 1.4 divide_subtract_fusion.2
  391.7 76.9 %reduce-scatter.16.cloned.1.call-done = f32[3,3,16,128]{3,2,1,0:T(8,128)} async-done(((f32[3,3,256,128]{3,2,1,0:T(8,128)}), f32[3,3,16,128]{3,2,1,0:T(8,128)}) %reduce-scatter.16.cloned.1.call-update) | async-done | bytes 73744 | tf_op jit(solution)/shard_map/reduce_scatter | solution.py:221
  468.6 1.6 divide_subtract_fusion
  470.2 76.7 %reduce-scatter.12.cloned.1.call-done = f32[3,3,16,128]{3,2,1,0:T(8,128)} async-done(((f32[3,3,256,128]{3,2,1,0:T(8,128)}), f32[3,3,16,128]{3,2,1,0:T(8,128)}) %reduce-scatter.12.cloned.1.call-update) | async-done | bytes 73744 | tf_op jit(solution)/shard_map/reduce_scatter | solution.py:220
  546.9 1.6 divide_subtract_fusion.1
  (227 shorter events, 35.2 us)
Async XLA Ops:
  7.2 102.9 %copy-start = (bf16[2,19,19,256]{3,0,2,1:T(2,128)(2,1)S(1)}, bf16[2,19,19,256]{3,0,2,1:T(2,128)(2,1)}, u32[]{:S(2)}) copy-start(bf16[2,19,19,256]{3,0,2,1:T(2,128)(2,1)} %param.16) | copy-start | bytes 1108996
  7.2 56.9 %copy-start.39 = (u32[32]{0:T(128)S(1)}, u32[32]{0:T(128)}, u32[]{:S(2)}) copy-start(u32[32]{0:T(128)} %constant.145) | copy-start | bytes 388
  7.2 54.9 %copy-start.37 = (s32[2,2]{1,0:T(2,128)S(1)}, s32[2,2]{1,0:T(2,128)}, u32[]{:S(2)}) copy-start(s32[2,2]{1,0:T(2,128)} %param.17) | copy-start | bytes 52
  7.2 56.8 %copy-start.29 = (f32[1,16]{1,0:T(1,128)S(1)}, f32[1,16]{1,0:T(1,128)}, u32[]{:S(2)}) copy-start(f32[1,16]{1,0:T(1,128)} %param.23) | copy-start | bytes 196
  7.2 150.1 %all-gather.4.cloned.1.call-start = ((), (), s32[]{:S(2)}) async-start(), calls=%async_computation.8 | async-start | bytes 1769472 | tf_op jit(solution)/shard_map/all_gather | solution.py:132
  58.3 52.6 %copy-start.18 = (f32[1,16,601]{2,1,0:T(8,128)S(1)}, f32[1,16,601]{2,1,0:T(8,128)}, u32[]{:S(2)}) copy-start(f32[1,16,601]{2,1,0:T(8,128)} %param.22) | copy-start | bytes 115396
  58.3 97.0 %all-to-all-start = ((bf16[16,3,3,16,128]{4,3,2,1,0:T(8,128)(2,1)}), bf16[16,3,3,16,128]{4,3,2,1,0:T(8,128)(2,1)S(1)}, u32[]{:S(2)}, u32[]{:S(2)}) async-start(bf16[16,3,3,16,128]{4,3,2,1,0:T(8,128)(2,1)} %stack.203), calls=%async_computation | async-start | bytes 1179648 | tf_op jit(solution)/shard_map/all_to_all | solution.py:123
  62.0 86.3 %copy-start.32 = (s32[2,2]{1,0:T(2,128)S(1)}, s32[2,2]{1,0:T(2,128)}, u32[]{:S(2)}) copy-start(s32[2,2]{1,0:T(2,128)} %param.19) | copy-start | bytes 52
  62.1 86.3 %copy-start.33 = (s32[2,2]{1,0:T(2,128)S(1)}, s32[2,2]{1,0:T(2,128)}, u32[]{:S(2)}) copy-start(s32[2,2]{1,0:T(2,128)} %param.18) | copy-start | bytes 52
  62.1 101.2 %all-gather.6.cloned.1.call-start = ((), (), s32[]{:S(2)}) async-start(), calls=%async_computation.9 | async-start | bytes 1769472 | tf_op jit(solution)/shard_map/all_gather | solution.py:133
  110.9 46.4 %copy-start.27 = (pred[8,3]{0,1:T(4,128)(4,1)S(1)}, pred[8,3]{0,1:T(4,128)(4,1)}, u32[]{:S(2)}) copy-start(pred[8,3]{0,1:T(4,128)(4,1)} %constant.135) | copy-start | bytes 76
  156.3 70.4 %reduce-scatter.18.cloned.1.call-start = ((), (), s32[]{:S(2)}) async-start(), calls=%async_computation.14 | async-start | bytes 1966080 | tf_op jit(solution)/shard_map/reduce_scatter | solution.py:216
  159.3 0.8 copy-start.9
  167.4 0.7 copy-start.1
  168.4 3.0 copy-start.36
  170.5 0.9 copy-start.11
  175.5 3.3 copy-start.12
  178.8 2.8 copy-start.34
  186.3 2.3 copy-start.7
  188.7 38.7 %reduce-scatter.14.cloned.1.call-start = ((), (), s32[]{:S(2)}) async-start(), calls=%async_computation.12 | async-start | bytes 3538944 | tf_op jit(solution)/shard_map/reduce_scatter | solution.py:215
  188.9 2.7 copy-start.16
  197.9 2.5 copy-start.3
  201.5 2.2 copy-start.17
  204.0 0.9 copy-start.4
  208.5 0.9 copy-start.8
  208.5 1.1 copy-start.10
  208.5 1.2 copy-start.20
  208.5 3.1 copy-start.6
  208.5 3.8 copy-start.15
  208.5 24.7 %reduce-scatter.10.cloned.1.call-start = ((), (), s32[]{:S(2)}) async-start(), calls=%async_computation.10 | async-start | bytes 3538944 | tf_op jit(solution)/shard_map/reduce_scatter | solution.py:214
  214.4 0.9 copy-start.2
  219.7 1.4 copy-start.35
  219.7 93.7 %reduce-scatter.22.cloned.1.call-start = ((), (), s32[]{:S(2)}) async-start(), calls=%async_computation.16 | async-start | bytes 139264
  222.3 91.8 %copy-start.30 = (f32[1,16]{1,0:T(1,128)S(1)}, f32[1,16]{1,0:T(1,128)}, u32[]{:S(2)}) copy-start(f32[1,16]{1,0:T(1,128)} %param.30) | copy-start | bytes 196
  222.3 91.8 %copy-start.31 = (f32[1,16]{1,0:T(1,128)S(1)}, f32[1,16]{1,0:T(1,128)}, u32[]{:S(2)}) copy-start(f32[1,16]{1,0:T(1,128)} %param.31) | copy-start | bytes 196
  222.3 167.9 %copy-start.19 = (f32[1,16,601]{2,1,0:T(8,128)S(1)}, f32[1,16,601]{2,1,0:T(8,128)}, u32[]{:S(2)}) copy-start(f32[1,16,601]{2,1,0:T(8,128)} %param.22) | copy-start | bytes 115396
  222.4 167.9 %copy-start.25 = (f32[1,16,601]{2,1,0:T(8,128)S(1)}, f32[1,16,601]{2,1,0:T(8,128)}, u32[]{:S(2)}) copy-start(f32[1,16,601]{2,1,0:T(8,128)} %param.28) | copy-start | bytes 115396
  222.4 167.9 %copy-start.26 = (f32[1,16,601]{2,1,0:T(8,128)S(1)}, f32[1,16,601]{2,1,0:T(8,128)}, u32[]{:S(2)}) copy-start(f32[1,16,601]{2,1,0:T(8,128)} %param.29) | copy-start | bytes 115396
  222.4 246.2 %copy-start.13 = (f32[3,3,16,128]{3,2,1,0:T(8,128)S(1)}, f32[3,3,16,128]{3,2,1,0:T(8,128)}, u32[]{:S(2)}) copy-start(f32[3,3,16,128]{3,2,1,0:T(8,128)} %param.21) | copy-start | bytes 221188
  222.4 246.2 %copy-start.21 = (f32[3,3,16,128]{3,2,1,0:T(8,128)S(1)}, f32[3,3,16,128]{3,2,1,0:T(8,128)}, u32[]{:S(2)}) copy-start(f32[3,3,16,128]{3,2,1,0:T(8,128)} %param.26) | copy-start | bytes 221188
  222.4 246.2 %copy-start.22 = (f32[3,3,16,128]{3,2,1,0:T(8,128)S(1)}, f32[3,3,16,128]{3,2,1,0:T(8,128)}, u32[]{:S(2)}) copy-start(f32[3,3,16,128]{3,2,1,0:T(8,128)} %param.27) | copy-start | bytes 221188
  222.4 324.5 %copy-start.14 = (f32[3,3,16,128]{3,2,1,0:T(8,128)S(1)}, f32[3,3,16,128]{3,2,1,0:T(8,128)}, u32[]{:S(2)}) copy-start(f32[3,3,16,128]{3,2,1,0:T(8,128)} %param.20) | copy-start | bytes 221188
  222.4 324.5 %copy-start.23 = (f32[3,3,16,128]{3,2,1,0:T(8,128)S(1)}, f32[3,3,16,128]{3,2,1,0:T(8,128)}, u32[]{:S(2)}) copy-start(f32[3,3,16,128]{3,2,1,0:T(8,128)} %param.24) | copy-start | bytes 221188
  222.4 324.5 %copy-start.24 = (f32[3,3,16,128]{3,2,1,0:T(8,128)S(1)}, f32[3,3,16,128]{3,2,1,0:T(8,128)}, u32[]{:S(2)}) copy-start(f32[3,3,16,128]{3,2,1,0:T(8,128)} %param.25) | copy-start | bytes 221188
  226.6 163.7 %reduce-scatter.20.cloned.1.call-start = ((), (), s32[]{:S(2)}) async-start(), calls=%async_computation.15 | async-start | bytes 696320 | tf_op jit(solution)/shard_map/reduce_scatter | solution.py:222
  227.3 241.3 %reduce-scatter.16.cloned.1.call-start = ((), (), s32[]{:S(2)}) async-start(), calls=%async_computation.13 | async-start | bytes 1253376 | tf_op jit(solution)/shard_map/reduce_scatter | solution.py:221
  228.1 318.9 %reduce-scatter.12.cloned.1.call-start = ((), (), s32[]{:S(2)}) async-start(), calls=%async_computation.11 | async-start | bytes 1253376 | tf_op jit(solution)/shard_map/reduce_scatter | solution.py:220
  314.2 234.4 %copy-start.28 = (f32[1,16]{1,0:T(1,128)}, f32[1,16]{1,0:T(1,128)S(1)}, u32[]{:S(2)}) copy-start(f32[1,16]{1,0:T(1,128)S(1)} %copy.110) | copy-start | bytes 196
  (2 other events, 1.4 us)
Sparse Core Ops, SparseCore 0:
  56.6 4.7 all-gather.3
  156.4 6.8 all-gather.5
  188.8 9.8 reduce-scatter.17
  208.6 11.1 reduce-scatter.13
  221.9 11.2 reduce-scatter.9
  235.3 78.0 reduce-scatter.21
  316.2 74.0 reduce-scatter.19
  393.1 75.4 reduce-scatter.15
  471.5 75.4 reduce-scatter.11
